TPU v7x, 32 devices: a whole 2x2x4 slice. The times are simulated.
32 devices in a mesh: dp: 8 (over z, x), tensor: 4 (over y, core).
Axes of the slice: x: 2, y: 2, z: 4, core: 2. Of those that a mesh axis runs over, the one named last changes fastest.
Arguments:
- residual_in: float32 [16384, 768], P(('dp', 'tensor')), may hold values from -6 to 6
- out_grad: float32 [16384, 768], P(('dp', 'tensor')), may hold values from -6 to 6
- seq_lengths: int32 [8, 16], P('dp'), may hold values from 0 to 1024, as said below
- timesteps: int32 [8, 16], P('dp'), may hold values from 0 to 1023
- norm_gain: float32 [768], replicated, may hold values from 0.5 to 1.5
- norm_bias: float32 [768], replicated, may hold values from -3 to 3
- qkv_weight: float32 [3, 768, 768], P(None, 'dp', 'tensor'), may hold values from -0.21875 to 0.21875
- proj_weight: float32 [768, 768], P('tensor', 'dp'), may hold values from -0.875 to 0.875
- proj_bias: float32 [768], replicated, may hold values from -2 to 2
- up_weight: float32 [768, 3072], P('dp', 'tensor'), may hold values from -0.21875 to 0.21875
- up_bias: float32 [3072], replicated, may hold values from -3 to 3
- down_weight: float32 [3072, 768], P('tensor', 'dp'), may hold values from -0.109375 to 0.109375
- down_bias: float32 [768], replicated, may hold values from -2 to 2
- time_weight: float32 [128, 2304], replicated, may hold values from -0.5 to 0.5
- time_bias: float32 [2304], replicated, may hold values from -3 to 3
Outputs:
- residual_out: float32 [16384, 768], P(('dp', 'tensor'))
- input_grad: float32 [16384, 768], P(('dp', 'tensor'))
- norm_gain_grad: float32 [768], replicated
- norm_bias_grad: float32 [768], replicated
- qkv_weight_grad: float32 [3, 768, 768], P(None, 'dp', 'tensor')
- proj_weight_grad: float32 [768, 768], P('tensor', 'dp')
- proj_bias_grad: float32 [768], replicated
- up_weight_grad: float32 [768, 3072], P('dp', 'tensor')
- up_bias_grad: float32 [3072], replicated
- down_weight_grad: float32 [3072, 768], P('tensor', 'dp')
- down_bias_grad: float32 [768], replicated
- time_weight_grad: float32 [128, 2304], replicated
- time_bias_grad: float32 [2304], replicated
Inputs may be any that keep to these rules, and one draw needn't show every extreme that they name: `seq_lengths`: row g lists the lengths of the sequences packed in order into the 2048 rows of pack g: the nonzero lengths come first and lie between 128 and 1024, their sum is at most 2048, the rows after it are padding, and every row holds a length of exactly 1024.
All inputs are finite; a program needn't handle non-finite values.
Results may differ from a plain program's by a relative error of at most 0.015.
Values may be sent and summed in bfloat16 or wider, within the bound.
A program may use at most 128 MiB of HBM per device.

v0:
```python
import math
import jax
import jax.numpy as jnp
from jax import lax
from jax.sharding import PartitionSpec as P

HDIM = 64
QBLK = 512
highest = lax.Precision.HIGHEST


def normalize(values):
    center = values - jnp.mean(values, axis=-1, keepdims=True)
    inverse = lax.rsqrt(jnp.mean(center * center, axis=-1, keepdims=True) + 1e-05)
    return (center * inverse, inverse)


def norm_back(grad_in, normed, inverse):
    return inverse * (
        grad_in
        - jnp.mean(grad_in, axis=-1, keepdims=True)
        - normed * jnp.mean(grad_in * normed, axis=-1, keepdims=True)
    )


def pack_info(lengths, row_total):
    row_index = jnp.arange(row_total, dtype=jnp.int32)
    seq_ends = jnp.cumsum(lengths)
    passed = row_index[:, None] >= seq_ends[None, :]
    segment = jnp.sum(passed.astype(jnp.int32), axis=1)
    starts = jnp.sum(jnp.where(passed, lengths[None, :], 0), axis=1)
    return (segment, row_index - starts)


def time_embed(time_index, embed_width):
    half_width = embed_width // 2
    freqs = jnp.exp(-math.log(10000.0) * jnp.arange(half_width, dtype=jnp.float32) / half_width)
    angles = time_index.astype(jnp.float32)[:, None] * freqs[None, :]
    return jnp.concatenate([jnp.cos(angles), jnp.sin(angles)], axis=1)


def rope_tables(positions, head_width):
    half_width = head_width // 2
    inverse = jnp.exp(
        -math.log(10000.0) * jnp.arange(half_width, dtype=jnp.float32) * (2.0 / head_width)
    )
    angles = positions.astype(jnp.float32)[:, None] * inverse[None, :]
    return (jnp.cos(angles)[:, None, :], jnp.sin(angles)[:, None, :])


def rotate(values, cosine, sine_table):
    half_width = values.shape[-1] // 2
    lead_half = values[..., :half_width]
    tail_half = values[..., half_width:]
    return jnp.concatenate(
        [lead_half * cosine - tail_half * sine_table, tail_half * cosine + lead_half * sine_table],
        axis=-1,
    )


def masked_scores(query_block, segment_block, keys_low, segment):
    scores = jnp.einsum("qhd,khd->hqk", query_block, keys_low, preferred_element_type=jnp.float32)
    allowed = segment_block[:, None] == segment[None, :]
    return jnp.where(allowed[None], scores, -1000000000.0)


def gelu_tanh(values):
    return jax.nn.gelu(values, approximate=True)


def shards(
    residual_in,
    out_grad,
    seq_lengths,
    timesteps,
    norm_gain,
    norm_bias,
    qkv_weight,
    proj_weight,
    proj_bias,
    up_weight,
    up_bias,
    down_weight,
    down_bias,
    time_weight,
    time_bias,
):
    row_count = residual_in.shape[0]
    width_model = residual_in.shape[1]
    tensor_size = lax.axis_size("tensor")
    tensor_rank = lax.axis_index("tensor")
    total_rows = row_count * tensor_size
    own_offset = tensor_rank * row_count
    segment, positions = pack_info(seq_lengths[0], total_rows)
    slot_count = seq_lengths.shape[1]
    own_segment = lax.dynamic_slice_in_dim(segment, own_offset, row_count)
    onehot = (own_segment[:, None] == jnp.arange(slot_count, dtype=jnp.int32)[None, :]).astype(
        jnp.float32
    )
    embedded = time_embed(timesteps[0], time_weight.shape[0])
    mod_table = jnp.dot(embedded, time_weight, precision=highest) + time_bias
    modulation = jnp.dot(onehot, mod_table, precision=highest)
    mod_scale = modulation[:, :width_model]
    mod_shift = modulation[:, width_model : 2 * width_model]
    mod_gate = modulation[:, 2 * width_model :]
    gathered_qkv, gathered_proj, gathered_up, gathered_down = (
        lax.all_gather(qkv_weight.astype(jnp.bfloat16), "dp", axis=1, tiled=True),
        lax.all_gather(proj_weight.astype(jnp.bfloat16), "dp", axis=1, tiled=True),
        lax.all_gather(up_weight.astype(jnp.bfloat16), "dp", axis=0, tiled=True),
        lax.all_gather(down_weight.astype(jnp.bfloat16), "dp", axis=1, tiled=True),
    )
    local_heads = gathered_qkv.shape[2] // HDIM
    local_units = gathered_up.shape[1]
    normed_in, inverse_in = normalize(residual_in)
    normed_low = (normed_in * norm_gain + norm_bias).astype(jnp.bfloat16)
    normed_full = lax.all_gather(normed_low, "tensor", axis=0, tiled=True)
    projected = jnp.einsum(
        "td,cde->cte", normed_full, gathered_qkv, preferred_element_type=jnp.float32
    )
    cosine, sine_table = rope_tables(positions, HDIM)
    head_scale = 1.0 / math.sqrt(HDIM)
    queries_low = (
        rotate(projected[0].reshape(total_rows, local_heads, HDIM), cosine, sine_table) * head_scale
    ).astype(jnp.bfloat16)
    keys_low = rotate(
        projected[1].reshape(total_rows, local_heads, HDIM), cosine, sine_table
    ).astype(jnp.bfloat16)
    values_low = projected[2].reshape(total_rows, local_heads, HDIM).astype(jnp.bfloat16)
    block_count = total_rows // QBLK
    query_blocks = queries_low.reshape(block_count, QBLK, local_heads, HDIM)
    segment_blocks = segment.reshape(block_count, QBLK)

    def forward_block(block_item):
        query_block, segment_block = block_item
        scores = masked_scores(query_block, segment_block, keys_low, segment)
        row_max = jnp.max(scores, axis=-1, keepdims=True)
        exponent = jnp.exp(scores - row_max)
        row_total = jnp.sum(exponent, axis=-1, keepdims=True)
        soft_weights = exponent / row_total
        mixed = jnp.einsum(
            "hqk,khd->qhd",
            soft_weights.astype(jnp.bfloat16),
            values_low,
            preferred_element_type=jnp.float32,
        )
        return (mixed.astype(jnp.bfloat16), (row_max + jnp.log(row_total))[..., 0])

    mixed_blocks, log_totals = lax.map(forward_block, (query_blocks, segment_blocks))
    mixed_flat = mixed_blocks.reshape(total_rows, local_heads * HDIM)
    attention = lax.psum_scatter(
        jnp.dot(mixed_flat, gathered_proj, preferred_element_type=jnp.float32).astype(jnp.bfloat16),
        "tensor",
        scatter_dimension=0,
        tiled=True,
    ).astype(jnp.float32)
    hidden = residual_in + attention + proj_bias
    hidden_normed, inverse_hidden = normalize(hidden)
    modulated_low = (hidden_normed * (1.0 + mod_scale) + mod_shift).astype(jnp.bfloat16)
    branch_grad = out_grad * mod_gate
    modulated_full = lax.all_gather(modulated_low, "tensor", axis=0, tiled=True)
    up_bias_own = lax.dynamic_slice_in_dim(up_bias, tensor_rank * local_units, local_units)
    pre_act = jnp.dot(modulated_full, gathered_up, preferred_element_type=jnp.float32) + up_bias_own
    active, gelu_pullback = jax.vjp(gelu_tanh, pre_act)
    active_low = active.astype(jnp.bfloat16)
    down_sum = lax.psum_scatter(
        jnp.dot(active_low, gathered_down, preferred_element_type=jnp.float32).astype(jnp.bfloat16),
        "tensor",
        scatter_dimension=0,
        tiled=True,
    ).astype(jnp.float32)
    branch = down_sum + down_bias
    residual_out = hidden + mod_gate * branch
    gate_grad = out_grad * branch
    branch_full = lax.all_gather(branch_grad.astype(jnp.bfloat16), "tensor", axis=0, tiled=True)
    down_part = lax.dot_general(
        active_low, branch_full, (((0,), (0,)), ((), ())), preferred_element_type=jnp.float32
    )
    active_grad = lax.dot_general(
        branch_full, gathered_down, (((1,), (1,)), ((), ())), preferred_element_type=jnp.float32
    )
    pre_grad = gelu_pullback(active_grad)[0].astype(jnp.bfloat16)
    up_bias_own_part = jnp.sum(pre_grad, axis=0, dtype=jnp.float32)
    up_bias_part = lax.dynamic_update_slice_in_dim(
        jnp.zeros(up_bias.shape, jnp.float32), up_bias_own_part, tensor_rank * local_units, 0
    )
    up_part = lax.dot_general(
        modulated_full, pre_grad, (((0,), (0,)), ((), ())), preferred_element_type=jnp.float32
    )
    modulated_grad = lax.psum_scatter(
        lax.dot_general(
            pre_grad, gathered_up, (((1,), (1,)), ((), ())), preferred_element_type=jnp.float32
        ).astype(jnp.bfloat16),
        "tensor",
        scatter_dimension=0,
        tiled=True,
    ).astype(jnp.float32)
    down_bias_part = jnp.sum(branch_grad, axis=0)
    scale_grad = modulated_grad * hidden_normed
    hidden_norm_grad = modulated_grad * (1.0 + mod_scale)
    hidden_grad = out_grad + norm_back(hidden_norm_grad, hidden_normed, inverse_hidden)
    mod_grad = jnp.concatenate([scale_grad, modulated_grad, gate_grad], axis=1)
    mod_seq_grad = lax.dot_general(onehot, mod_grad, (((0,), (0,)), ((), ())), precision=highest)
    time_weight_part = lax.dot_general(
        embedded, mod_seq_grad, (((0,), (0,)), ((), ())), precision=highest
    )
    time_bias_part = jnp.sum(mod_seq_grad, axis=0)
    proj_bias_part = jnp.sum(hidden_grad, axis=0)
    hidden_full = lax.all_gather(hidden_grad.astype(jnp.bfloat16), "tensor", axis=0, tiled=True)
    proj_part = lax.dot_general(
        mixed_flat, hidden_full, (((0,), (0,)), ((), ())), preferred_element_type=jnp.float32
    )
    mixed_grad = lax.dot_general(
        hidden_full, gathered_proj, (((1,), (1,)), ((), ())), preferred_element_type=jnp.float32
    )
    grad_blocks = mixed_grad.astype(jnp.bfloat16).reshape(block_count, QBLK, local_heads, HDIM)

    def backward_block(carried, block_item):
        key_sum, value_sum = carried
        query_block, segment_block, log_block, grad_block = block_item
        scores = masked_scores(query_block, segment_block, keys_low, segment)
        soft_weights = jnp.exp(scores - log_block[:, :, None])
        prob_grad = jnp.einsum(
            "qhd,khd->hqk", grad_block, values_low, preferred_element_type=jnp.float32
        )
        row_inner = jnp.sum(soft_weights * prob_grad, axis=-1, keepdims=True)
        score_grad = (soft_weights * (prob_grad - row_inner)).astype(jnp.bfloat16)
        query_grad = jnp.einsum(
            "hqk,khd->qhd", score_grad, keys_low, preferred_element_type=jnp.float32
        )
        key_sum = key_sum + jnp.einsum(
            "hqk,qhd->khd", score_grad, query_block, preferred_element_type=jnp.float32
        )
        value_sum = value_sum + jnp.einsum(
            "hqk,qhd->khd",
            soft_weights.astype(jnp.bfloat16),
            grad_block,
            preferred_element_type=jnp.float32,
        )
        return ((key_sum, value_sum), query_grad)

    empty_grad = jnp.zeros((total_rows, local_heads, HDIM), jnp.float32)
    (key_grad, value_grad), query_grads = lax.scan(
        backward_block,
        (empty_grad, empty_grad),
        (query_blocks, segment_blocks, log_totals, grad_blocks),
    )
    query_grad_all = query_grads.reshape(total_rows, local_heads, HDIM)
    query_raw_grad = rotate(query_grad_all * head_scale, cosine, -sine_table)
    key_raw_grad = rotate(key_grad, cosine, -sine_table)
    qkv_grad = (
        jnp.stack([query_raw_grad, key_raw_grad, value_grad])
        .reshape(3, total_rows, local_heads * HDIM)
        .astype(jnp.bfloat16)
    )
    qkv_part = jnp.einsum("td,cte->cde", normed_full, qkv_grad, preferred_element_type=jnp.float32)
    normed_grad = lax.psum_scatter(
        jnp.einsum(
            "cte,cde->td", qkv_grad, gathered_qkv, preferred_element_type=jnp.float32
        ).astype(jnp.bfloat16),
        "tensor",
        scatter_dimension=0,
        tiled=True,
    ).astype(jnp.float32)
    gain_part = jnp.sum(normed_grad * normed_in, axis=0)
    bias_part = jnp.sum(normed_grad, axis=0)
    input_grad = hidden_grad + norm_back(normed_grad * norm_gain, normed_in, inverse_in)
    grad_qkv, grad_proj, grad_up, grad_down = (
        lax.psum_scatter(qkv_part, "dp", scatter_dimension=1, tiled=True),
        lax.psum_scatter(proj_part, "dp", scatter_dimension=1, tiled=True),
        lax.psum_scatter(up_part, "dp", scatter_dimension=0, tiled=True),
        lax.psum_scatter(down_part, "dp", scatter_dimension=1, tiled=True),
    )
    small_sums = lax.psum(
        (
            gain_part,
            bias_part,
            proj_bias_part,
            up_bias_part,
            down_bias_part,
            time_weight_part,
            time_bias_part,
        ),
        ("dp", "tensor"),
    )
    return (
        residual_out,
        input_grad,
        small_sums[0],
        small_sums[1],
        grad_qkv,
        grad_proj,
        small_sums[2],
        grad_up,
        small_sums[3],
        grad_down,
        small_sums[4],
        small_sums[5],
        small_sums[6],
    )


def solution(mesh):
    in_specs = (
        P(("dp", "tensor"), None),
        P(("dp", "tensor"), None),
        P("dp", None),
        P("dp", None),
        P(),
        P(),
        P(None, "dp", "tensor"),
        P("tensor", "dp"),
        P(),
        P("dp", "tensor"),
        P(),
        P("tensor", "dp"),
        P(),
        P(),
        P(),
    )
    out_specs = (
        P(("dp", "tensor"), None),
        P(("dp", "tensor"), None),
        P(),
        P(),
        P(None, "dp", "tensor"),
        P("tensor", "dp"),
        P(),
        P("dp", "tensor"),
        P(),
        P("tensor", "dp"),
        P(),
        P(),
        P(),
    )
    return jax.shard_map(shards, mesh=mesh, in_specs=in_specs, out_specs=out_specs, check_vma=False)
```

profile of v0, /device:TPU:0, one launch (start us, length us, event | category | flops | bytes accessed | tf_op | source)
XLA Modules:
  0.0 983.2 jit_solution(7752783415744753247)
XLA Ops:
  12.9 40.6 %all_gather.25 = bf16[3,768,192]{2,0,1:T(4,128)(2,1)} all-gather(bf16[3,96,192]{2,0,1:T(4,128)(2,1)S(1)} %copy.65), channel_id=1, replica_groups=mesh['dp'=8,'tensor'=4] {'dp'}, dimensions={1}, use_global_device_ids=true | all-gather | bytes 995328 | tf_op jit(solution)/shard_map/all_gather | solution.py:107
  57.0 33.0 %all_gather.26 = bf16[192,768]{0,1:T(8,128)(2,1)} all-gather(bf16[192,96]{0,1:T(8,128)(2,1)S(1)} %copy.69), channel_id=1, replica_groups=mesh['dp'=8,'tensor'=4] {'dp'}, dimensions={1}, use_global_device_ids=true | all-gather | bytes 331776 | tf_op jit(solution)/shard_map/all_gather | solution.py:108
  106.1 95.3 %while.27 = (s32[]{:T(128)}, bf16[4,512,3,64]{1,3,2,0:T(8,128)(2,1)}, f32[4,3,512]{2,1,0:T(4,128)}, s32[4,512]{1,0:T(4,128)S(1)}, s32[2048]{0:T(1024)S(1)}, /*in...) while((s32[]{:T(128)}, ...), condition=%wide.region_8.9_spmd, body=%wide.region_5.8_spmd.sunk | while | flops 834763264 | bytes 47120528 | solution.py:148
  107.0 7.6 select_reduce_fusion.3
  114.6 7.8 fusion.140
  122.4 7.1 fusion.141
  130.7 7.6 select_reduce_fusion.3
  138.3 7.8 fusion.140
  146.1 7.1 fusion.141
  154.5 7.6 select_reduce_fusion.3
  162.1 7.8 fusion.140
  169.9 7.1 fusion.141
  178.2 7.6 select_reduce_fusion.3
  185.8 7.8 fusion.140
  193.7 7.1 fusion.141
  218.0 26.7 %reduce-scatter.13.cloned.1.call-done = bf16[512,768]{1,0:T(8,128)(2,1)} async-done(((bf16[2048,768]{1,0:T(8,128)(2,1)}), bf16[512,768]{1,0:T(8,128)(2,1)}) %reduce-scatter.13.cloned.1.call-update) | async-done | bytes 786448 | tf_op jit(solution)/shard_map/reduce_scatter | solution.py:150
  252.9 27.2 %all-gather.9.cloned.1.call-done = bf16[2048,768]{1,0:T(8,128)(2,1)} async-done(((bf16[512,768]{1,0:T(8,128)(2,1)}), bf16[2048,768]{1,0:T(8,128)(2,1)}) %all-gather.9.cloned.1.call-update) | async-done | bytes 3145744 | tf_op jit(solution)/shard_map/all_gather | solution.py:160
  280.1 7.5 fusion.88
  287.6 36.0 %all-gather.13.cloned.1.call-done = bf16[768,768]{0,1:T(8,128)(2,1)} async-done(((bf16[768,96]{0,1:T(8,128)(2,1)}), bf16[768,768]{0,1:T(8,128)(2,1)}) %all-gather.13.cloned.1.call-update) | async-done | bytes 1179664 | tf_op jit(solution)/shard_map/all_gather | solution.py:110
  323.6 28.9 %all-gather.15.cloned.1.call-done = bf16[2048,768]{1,0:T(8,128)(2,1)} async-done(((bf16[512,768]{1,0:T(8,128)(2,1)}), bf16[2048,768]{1,0:T(8,128)(2,1)}) %all-gather.15.cloned.1.call-update) | async-done | bytes 3145744 | tf_op jit(solution)/shard_map/all_gather | solution.py:174
  352.6 10.8 %convert_reduce_fusion = (f32[768]{0:T(1024)}, bf16[2048,768]{1,0:T(8,128)(2,1)S(1)}, bf16[2048,768]{1,0:T(8,128)(2,1)}) fusion(f32[2048,768]{1,0:T(8,128)} %fusion.88, f32[768]{0:T(1024)S(1)} %dynamic_slice.28, bf16[2048,768]{1,0:T(8,128)(2,1)} %all-gather.15.cloned.1.call-done, bf16[768,768]{0,1:T(8,128)(2,1)} %all-gather.13.cloned.1.call-done), kind=kOutput, calls=%fused_computation.57 | convolution fusion | flops 2455239936 | bytes 16914432 | tf_op jit(solution)/shard_map/dot_general | solution.py:178
  370.3 6.2 convolution_convert_fusion.1
  376.6 30.5 %reduce-scatter.17.cloned.1.call-done = bf16[512,768]{1,0:T(8,128)(2,1)} async-done(((bf16[2048,768]{1,0:T(8,128)(2,1)}), bf16[512,768]{1,0:T(8,128)(2,1)}) %reduce-scatter.17.cloned.1.call-update) | async-done | bytes 786448 | tf_op jit(solution)/shard_map/reduce_scatter | solution.py:189
  411.1 36.4 %reduce-scatter.15.cloned.1.call-done = bf16[512,768]{1,0:T(8,128)(2,1)} async-done(((bf16[2048,768]{1,0:T(8,128)(2,1)}), bf16[512,768]{1,0:T(8,128)(2,1)}) %reduce-scatter.15.cloned.1.call-update) | async-done | bytes 786448 | tf_op jit(solution)/shard_map/reduce_scatter | solution.py:165
  454.8 28.4 %all-gather.17.cloned.1.call-done = bf16[2048,768]{1,0:T(8,128)(2,1)} async-done(((bf16[512,768]{1,0:T(8,128)(2,1)}), bf16[2048,768]{1,0:T(8,128)(2,1)}) %all-gather.17.cloned.1.call-update) | async-done | bytes 3145744 | tf_op jit(solution)/shard_map/all_gather | solution.py:208
  487.0 157.7 %while.28 = (s32[]{:T(128)}, f32[2048,3,64]{0,2,1:T(8,128)}, f32[2048,3,64]{0,2,1:T(8,128)}, f32[4,512,3,64]{1,0,3,2:T(4,128)}, bf16[4,512,3,64]{1,3,2,0:T(8,128...) while((s32[]{:T(128)}, f32[2048,3,64]{0,2,1:T(8,128)}, ...), condition=%wide.region_18.19_spmd.clone, body=%wide.region_16.18_spmd.clone.sunk | while | flops 2053634560 | bytes 151972176 | solution.py:242
  501.4 5.9 multiply_convert_fusion.3
  516.4 8.6 dynamic_update_slice.24
  529.5 5.8 fusion.153
  535.3 5.4 multiply_reduce_fusion.5
  540.7 5.9 multiply_convert_fusion.3
  556.3 8.6 dynamic_update_slice.24
  569.3 5.8 fusion.153
  575.1 5.4 multiply_reduce_fusion.5
  580.5 5.9 multiply_convert_fusion.3
  596.1 8.6 dynamic_update_slice.24
  609.2 5.8 fusion.153
  620.4 5.9 multiply_convert_fusion.3
  635.9 8.6 dynamic_update_slice.24
  668.3 5.7 bitcast_convert_fusion
  675.9 6.0 fusion.89
  682.2 6.9 fusion.90
  696.3 19.6 %reduce-scatter.27.cloned.1.call-done = f32[96,192]{1,0:T(8,128)} async-done(((f32[768,192]{1,0:T(8,128)}), f32[96,192]{1,0:T(8,128)}) %reduce-scatter.27.cloned.1.call-update) | async-done | bytes 73744
  717.5 68.3 %reduce-scatter.25.cloned.1.call-done = f32[96,576]{1,0:T(8,128)} async-done(((f32[768,576]{1,0:T(8,128)}), f32[96,576]{1,0:T(8,128)}) %reduce-scatter.25.cloned.1.call-update) | async-done | bytes 221200
  787.7 37.6 %reduce-scatter.19.cloned.1.call-done = bf16[512,768]{1,0:T(8,128)(2,1)} async-done(((bf16[2048,768]{1,0:T(8,128)(2,1)}), bf16[512,768]{1,0:T(8,128)(2,1)}) %reduce-scatter.19.cloned.1.call-update) | async-done | bytes 786448 | tf_op jit(solution)/shard_map/reduce_scatter | solution.py:256
  827.8 41.3 %all-reduce = (f32[768]{0:T(1024)}, f32[768]{0:T(1024)}, f32[768]{0:T(1024)}, f32[3072]{0:T(1024)}, f32[768]{0:T(1024)}, /*index=5*/f32[2304]{0:T(1024)}) all-reduce(f32[768]{0:T(1024)S(1)} %get-tuple-element.311, f32[768]{0:T(1024)S(1)} %get-tuple-element.314, ...), channel_id=1, replica_groups=mesh['dp'=8,'tensor'=4] {'dp','tensor'}, use_global_device_ids=true, to_apply=%region_23.24 | all-reduce | flops 8448 | bytes 67584 | tf_op jit(solution)/shard_map/psum | solution.py:273
  872.3 27.9 %reduce-scatter.21.cloned.1.call-done = f32[96,768]{1,0:T(8,128)} async-done(((f32[768,768]{1,0:T(8,128)}), f32[96,768]{1,0:T(8,128)}) %reduce-scatter.21.cloned.1.call-update) | async-done | bytes 294928 | tf_op jit(solution)/shard_map/reduce_scatter | solution.py:270
  900.2 73.0 %reduce-scatter.23.cloned.1.call-done = f32[768,96]{0,1:T(8,128)} async-done(((f32[768,768]{0,1:T(8,128)}), f32[768,96]{0,1:T(8,128)}) %reduce-scatter.23.cloned.1.call-update) | async-done | bytes 294928 | tf_op jit(solution)/shard_map/reduce_scatter | solution.py:271
  (317 shorter events, 191.2 us)
Async XLA Ops:
  8.0 204.3 %copy-start = (f32[128,2304]{1,0:T(8,128)S(1)}, f32[128,2304]{1,0:T(8,128)}, u32[]{:S(2)}) copy-start(f32[128,2304]{1,0:T(8,128)} %param.32) | copy-start | bytes 3538948
  8.1 83.6 %all-gather.7.cloned.1.call-start = ((), (), s32[]{:S(2)}) async-start(), calls=%async_computation.8 | async-start | bytes 3932160 | tf_op jit(solution)/shard_map/all_gather | solution.py:116
  11.6 233.2 %reduce-scatter.13.cloned.1.call-start = ((), (), s32[]{:S(2)}) async-start(), calls=%async_computation.9 | async-start | bytes 3932160 | tf_op jit(solution)/shard_map/reduce_scatter | solution.py:150
  53.5 36.4 %copy-start.45 = (s32[2048]{0:T(1024)S(1)}, s32[2048]{0:T(1024)}, u32[]{:S(2)}) copy-start(s32[2048]{0:T(1024)} %get-tuple-element.315) | copy-start | bytes 24580
  91.7 5.6 copy-start.22
  114.6 7.8 copy-start.10
  138.3 7.8 copy-start.10
  162.1 7.8 copy-start.10
  185.8 7.8 copy-start.10
  206.9 46.0 %all-gather.11.cloned.1.call-start = ((), (), s32[]{:S(2)}) async-start(), calls=%async_computation.11 | async-start | bytes 1327104 | tf_op jit(solution)/shard_map/all_gather | solution.py:109
  208.6 71.5 %all-gather.9.cloned.1.call-start = ((), (), s32[]{:S(2)}) async-start(), calls=%async_computation.10 | async-start | bytes 3932160 | tf_op jit(solution)/shard_map/all_gather | solution.py:160
  213.7 31.1 %copy-start.52 = (f32[768]{0:T(1024)S(1)}, f32[768]{0:T(1024)}, u32[]{:S(2)}) copy-start(f32[768]{0:T(1024)} %param.27) | copy-start | bytes 9220
  250.6 73.1 %all-gather.13.cloned.1.call-start = ((), (), s32[]{:S(2)}) async-start(), calls=%async_computation.12 | async-start | bytes 1327104 | tf_op jit(solution)/shard_map/all_gather | solution.py:110
  251.3 101.2 %all-gather.15.cloned.1.call-start = ((), (), s32[]{:S(2)}) async-start(), calls=%async_computation.14 | async-start | bytes 3932160 | tf_op jit(solution)/shard_map/all_gather | solution.py:174
  252.1 155.1 %reduce-scatter.17.cloned.1.call-start = ((), (), s32[]{:S(2)}) async-start(), calls=%async_computation.15 | async-start | bytes 3932160 | tf_op jit(solution)/shard_map/reduce_scatter | solution.py:189
  287.6 77.4 %copy-start.57 = (bf16[768,768]{1,0:T(8,128)(2,1)S(1)}, bf16[768,768]{1,0:T(8,128)(2,1)}, u32[]{:S(2)}) copy-start(bf16[768,768]{1,0:T(8,128)(2,1)} %all-gather.11.cloned.1.call-done) | copy-start | bytes 3538948
  369.1 78.3 %reduce-scatter.15.cloned.1.call-start = ((), (), s32[]{:S(2)}) async-start(), calls=%async_computation.13 | async-start | bytes 3932160 | tf_op jit(solution)/shard_map/reduce_scatter | solution.py:165
  376.6 30.6 %copy-start.12 = (f32[512,768]{1,0:T(8,128)S(1)}, f32[512,768]{1,0:T(8,128)}, u32[]{:S(2)}) copy-start(f32[512,768]{1,0:T(8,128)} %copy-done.11) | copy-start | bytes 4718596
  376.6 70.9 %copy-start.53 = (f32[768]{0:T(1024)S(1)}, f32[768]{0:T(1024)}, u32[]{:S(2)}) copy-start(f32[768]{0:T(1024)} %param.31) | copy-start | bytes 9220
  376.6 106.6 %all-gather.17.cloned.1.call-start = ((), (), s32[]{:S(2)}) async-start(), calls=%async_computation.16 | async-start | bytes 3932160 | tf_op jit(solution)/shard_map/all_gather | solution.py:208
  407.1 40.3 %copy-start.16 = (bf16[512,768]{1,0:T(8,128)(2,1)S(1)}, bf16[512,768]{1,0:T(8,128)(2,1)}, u32[]{:S(2)}) copy-start(bf16[512,768]{1,0:T(8,128)(2,1)} %reduce-scatter.17.cloned.1.call-done) | copy-start | bytes 2359300
  452.5 30.6 %copy-start.19 = (bf16[192,768]{0,1:T(8,128)(2,1)S(1)}, bf16[192,768]{0,1:T(8,128)(2,1)}, u32[]{:S(2)}) copy-start(bf16[192,768]{0,1:T(8,128)(2,1)} %all_gather.26) | copy-start | bytes 884740
  454.7 261.2 %reduce-scatter.27.cloned.1.call-start = ((), (), s32[]{:S(2)}) async-start(), calls=%async_computation.22 | async-start | bytes 884736
  507.3 5.1 copy-start.2
  512.4 12.6 %copy-start.5 = (bf16[2048,3,64]{0,2,1:T(8,128)(2,1)S(1)}, bf16[2048,3,64]{0,2,1:T(8,128)(2,1)}, u32[]{:S(2)}) copy-start(bf16[2048,3,64]{0,2,1:T(8,128)(2,1)} %copy-done.4) | copy-start | bytes 2359300 | tf_op jit(solution)/shard_map/while
  512.5 12.6 %copy-start.15 = (bf16[4,512,3,64]{1,3,2,0:T(8,128)(2,1)S(1)}, bf16[4,512,3,64]{1,3,2,0:T(8,128)(2,1)}, u32[]{:S(2)}) copy-start(bf16[4,512,3,64]{1,3,2,0:T(8,128)(2,1)} %copy-done.14) | copy-start | bytes 2359300 | tf_op jit(solution)/shard_map/while
  546.6 5.1 copy-start.2
  551.7 13.2 %copy-start.5 = (bf16[2048,3,64]{0,2,1:T(8,128)(2,1)S(1)}, bf16[2048,3,64]{0,2,1:T(8,128)(2,1)}, u32[]{:S(2)}) copy-start(bf16[2048,3,64]{0,2,1:T(8,128)(2,1)} %copy-done.4) | copy-start | bytes 2359300 | tf_op jit(solution)/shard_map/while
  551.7 13.1 %copy-start.15 = (bf16[4,512,3,64]{1,3,2,0:T(8,128)(2,1)S(1)}, bf16[4,512,3,64]{1,3,2,0:T(8,128)(2,1)}, u32[]{:S(2)}) copy-start(bf16[4,512,3,64]{1,3,2,0:T(8,128)(2,1)} %copy-done.14) | copy-start | bytes 2359300 | tf_op jit(solution)/shard_map/while
  586.4 5.1 copy-start.2
  591.5 13.2 %copy-start.5 = (bf16[2048,3,64]{0,2,1:T(8,128)(2,1)S(1)}, bf16[2048,3,64]{0,2,1:T(8,128)(2,1)}, u32[]{:S(2)}) copy-start(bf16[2048,3,64]{0,2,1:T(8,128)(2,1)} %copy-done.4) | copy-start | bytes 2359300 | tf_op jit(solution)/shard_map/while
  591.5 13.1 %copy-start.15 = (bf16[4,512,3,64]{1,3,2,0:T(8,128)(2,1)S(1)}, bf16[4,512,3,64]{1,3,2,0:T(8,128)(2,1)}, u32[]{:S(2)}) copy-start(bf16[4,512,3,64]{1,3,2,0:T(8,128)(2,1)} %copy-done.14) | copy-start | bytes 2359300 | tf_op jit(solution)/shard_map/while
  626.2 5.1 copy-start.2
  631.4 13.2 %copy-start.5 = (bf16[2048,3,64]{0,2,1:T(8,128)(2,1)S(1)}, bf16[2048,3,64]{0,2,1:T(8,128)(2,1)}, u32[]{:S(2)}) copy-start(bf16[2048,3,64]{0,2,1:T(8,128)(2,1)} %copy-done.4) | copy-start | bytes 2359300 | tf_op jit(solution)/shard_map/while
  631.4 13.1 %copy-start.15 = (bf16[4,512,3,64]{1,3,2,0:T(8,128)(2,1)S(1)}, bf16[4,512,3,64]{1,3,2,0:T(8,128)(2,1)}, u32[]{:S(2)}) copy-start(bf16[4,512,3,64]{1,3,2,0:T(8,128)(2,1)} %copy-done.14) | copy-start | bytes 2359300 | tf_op jit(solution)/shard_map/while
  652.1 133.7 %reduce-scatter.25.cloned.1.call-start = ((), (), s32[]{:S(2)}) async-start(), calls=%async_computation.21 | async-start | bytes 2211840
  666.9 158.4 %reduce-scatter.19.cloned.1.call-start = ((), (), s32[]{:S(2)}) async-start(), calls=%async_computation.17 | async-start | bytes 3932160 | tf_op jit(solution)/shard_map/reduce_scatter | solution.py:256
  674.0 226.3 %reduce-scatter.21.cloned.1.call-start = ((), (), s32[]{:S(2)}) async-start(), calls=%async_computation.18 | async-start | bytes 2654208 | tf_op jit(solution)/shard_map/reduce_scatter | solution.py:270
  681.9 291.4 %reduce-scatter.23.cloned.1.call-start = ((), (), s32[]{:S(2)}) async-start(), calls=%async_computation.19 | async-start | bytes 2654208 | tf_op jit(solution)/shard_map/reduce_scatter | solution.py:271
  689.2 284.1 %all-reduce.3.cloned.1.call-start = ((), (), s32[]{:S(2)}) async-start(), calls=%async_computation.20 | async-start | bytes 2359296 | tf_op jit(solution)/shard_map/psum | solution.py:273
  694.0 131.3 %copy-start.8 = (f32[512,768]{1,0:T(8,128)S(1)}, f32[512,768]{1,0:T(8,128)}, u32[]{:S(2)}) copy-start(f32[512,768]{1,0:T(8,128)} %param.19) | copy-start | bytes 4718596
  694.0 131.3 %copy-start.40 = (f32[512]{0:T(512)S(1)}, f32[512]{0:T(512)}, u32[]{:S(2)}) copy-start(f32[512]{0:T(512)} %copy-done.39) | copy-start | bytes 6148
  694.0 131.2 %copy-start.42 = (f32[768]{0:T(1024)S(1)}, f32[768]{0:T(1024)}, u32[]{:S(2)}) copy-start(f32[768]{0:T(1024)} %param.23) | copy-start | bytes 9220
  694.0 131.2 %copy-start.44 = (f32[512]{0:T(512)S(1)}, f32[512]{0:T(512)}, u32[]{:S(2)}) copy-start(f32[512]{0:T(512)} %copy-done.43) | copy-start | bytes 6148
  717.5 110.3 %copy-start.46 = (f32[768]{0:T(1024)S(1)}, f32[768]{0:T(1024)}, u32[]{:S(2)}) copy-start(f32[768]{0:T(1024)} %get-tuple-element.310) | copy-start | bytes 9220
  717.5 110.3 %copy-start.47 = (f32[768]{0:T(1024)S(1)}, f32[768]{0:T(1024)}, u32[]{:S(2)}) copy-start(f32[768]{0:T(1024)} %get-tuple-element.363) | copy-start | bytes 9220
  825.3 43.9 %copy-start.20 = (bf16[512,768]{1,0:T(8,128)(2,1)S(1)}, bf16[512,768]{1,0:T(8,128)(2,1)}, u32[]{:S(2)}) copy-start(bf16[512,768]{1,0:T(8,128)(2,1)} %reduce-scatter.19.cloned.1.call-done) | copy-start | bytes 2359300
  869.1 106.5 %copy-start.1 = (f32[128,2304]{1,0:T(8,128)S(1)}, f32[128,2304]{1,0:T(8,128)}, u32[]{:S(2)}) copy-start(f32[128,2304]{1,0:T(8,128)} %param.32) | copy-start | bytes 3538948
  (48 other events, 122.7 us)
Sparse Core Ops, SparseCore 0:
  11.7 31.2 all-gather.6
  207.0 37.6 reduce-scatter.12
  369.2 37.8 reduce-scatter.16
  409.5 37.8 reduce-scatter.14
  696.4 151.9 all-reduce.2
Sparse Core Ops, SparseCore 1:
  210.2 41.1 all-gather.10
  253.3 26.7 all-gather.8
  282.2 41.4 all-gather.12
  325.8 26.7 all-gather.14
  454.8 28.3 all-gather.16
  652.2 63.6 reduce-scatter.26
  719.2 66.5 reduce-scatter.24
  788.2 37.0 reduce-scatter.18
  829.2 71.0 reduce-scatter.20
  904.3 68.9 reduce-scatter.22
where the time goes:
time: 991 us; the launch traced here: 983 us
  waiting for transfers between devices  441 us (45%)
  matrix products  226 us (23%)
  blocking collectives  115 us (12%)
  other arithmetic  102 us (10%)
  local copies, waits for them, and re-layouts  79.7 us (8%)
  between operations  16.4 us (2%)
    unnamed x17, waiting for transfers between devices  88.8 us
    reduce_scatter x1, waiting for transfers between devices, shards(): lax.psum_scatter(down_part, 'dp', scatter_dimension=1, tiled=True)  73 us
    dot_general x8, matrix products, masked_scores(): jnp.einsum('qhd,khd->hqk', query_block, keys_low, preferred_element_type=...  42.3 us
    psum x1, blocking collectives, shards(): lax.psum((gain_part, bias_part, proj_bias_part, up_bias_part, down_bias_p...  41.3 us
    all_gather x1, blocking collectives, shards(): lax.all_gather(qkv_weight.astype(jnp.bfloat16), 'dp', axis=1, tiled=True)  40.6 us
    reduce_scatter x1, waiting for transfers between devices, shards(): lax.psum_scatter(jnp.einsum('cte,cde->td', qkv_grad, gathered_qkv, prefer...  37.6 us
    reduce_scatter x1, waiting for transfers between devices, shards(): lax.psum_scatter(jnp.dot(active_low, gathered_down, preferred_element_typ...  36.4 us
    dynamic_update_slice x8, local copies, waits for them, and re-layouts, shards(): lax.scan(backward_block, (empty_grad, empty_grad), (query_blocks, segment...  36 us
  transfers between devices with their start and end apart: 15, of which 12 were waited for; matrix products, arithmetic and copies ran while one was open for 9% of the time, Pallas kernels for 0%

commit v1 on v0

--- a/solution.py
+++ b/solution.py
@@ -7,6 +7,28 @@
 HDIM = 64
 QBLK = 512
 highest = lax.Precision.HIGHEST
+
+
+def joined_along(blocks, dim):
+    blocks = jnp.moveaxis(blocks, 0, dim)
+    lengths = blocks.shape
+    return blocks.reshape(*lengths[:dim], lengths[dim] * lengths[dim + 1], *lengths[dim + 2 :])
+
+
+def grow_blocks(x, axis):
+    size = lax.axis_size(axis)
+    blocks = x[None]
+    for level in range(size.bit_length() - 1):
+        apart = 1 << level
+        other = lax.ppermute(blocks, axis, [(i, i ^ apart) for i in range(size)])
+        both = jnp.stack([blocks, other])
+        upper = lax.axis_index(axis) >> level & 1
+        blocks = jnp.where(upper == 0, both, both[::-1]).reshape(-1, *x.shape)
+    return blocks
+
+
+def doubled_up(value, axis, dim):
+    return joined_along(grow_blocks(value, axis), dim)
 
 
 def normalize(values):
@@ -105,7 +127,7 @@
     mod_gate = modulation[:, 2 * width_model :]
     gathered_qkv, gathered_proj, gathered_up, gathered_down = (
         lax.all_gather(qkv_weight.astype(jnp.bfloat16), "dp", axis=1, tiled=True),
-        lax.all_gather(proj_weight.astype(jnp.bfloat16), "dp", axis=1, tiled=True),
+        doubled_up(proj_weight.astype(jnp.bfloat16), "dp", 1),
         lax.all_gather(up_weight.astype(jnp.bfloat16), "dp", axis=0, tiled=True),
         lax.all_gather(down_weight.astype(jnp.bfloat16), "dp", axis=1, tiled=True),
     )

time: 991 us -> 961 us (0.970)
  blocking collectives: 115 us -> 77.7 us
    all_gather x1 -> x0, blocking collectives: 33 us -> none  [shards(): lax.all_gather(proj_weight.astype(jnp.bfloat16), 'dp', axis=1, tiled=True)]
    unnamed x115 -> x130, local copies, waits for them, and re-layouts: 25.8 us -> 28 us
  transfers between devices with their start and end apart: 15 -> 18, of which waited for: 12 -> 14; matrix products, arithmetic and copies ran while one was open for 9% -> 9% of each run, Pallas kernels for 0% -> 0%
where the time goes in v1:
time: 961 us; the launch traced here: 953 us
  waiting for transfers between devices  445 us (46%)
  matrix products  225 us (23%)
  other arithmetic  97.2 us (10%)
  local copies, waits for them, and re-layouts  80.3 us (8%)
  blocking collectives  77.7 us (8%)
  between operations  16.5 us (2%)
  starting transfers between devices  9.66 us (1%)
    unnamed x17, waiting for transfers between devices  88.8 us
    reduce_scatter x1, waiting for transfers between devices, shards(): lax.psum_scatter(down_part, 'dp', scatter_dimension=1, tiled=True)  72.9 us
    dot_general x8, matrix products, masked_scores(): jnp.einsum('qhd,khd->hqk', query_block, keys_low, preferred_element_type=...  42.4 us
    psum x1, blocking collectives, shards(): lax.psum((gain_part, bias_part, proj_bias_part, up_bias_part, down_bias_p...  41.6 us
    reduce_scatter x1, waiting for transfers between devices, shards(): lax.psum_scatter(jnp.einsum('cte,cde->td', qkv_grad, gathered_qkv, prefer...  37.5 us
    reduce_scatter x1, waiting for transfers between devices, shards(): lax.psum_scatter(jnp.dot(active_low, gathered_down, preferred_element_typ...  36.4 us
    all_gather x1, blocking collectives, shards(): lax.all_gather(qkv_weight.astype(jnp.bfloat16), 'dp', axis=1, tiled=True)  36.1 us
    dynamic_update_slice x8, local copies, waits for them, and re-layouts, shards(): lax.scan(backward_block, (empty_grad, empty_grad), (query_blocks, segment...  36 us
  transfers between devices with their start and end apart: 18, of which 14 were waited for; matrix products, arithmetic and copies ran while one was open for 9% of the time, Pallas kernels for 0%

profile of v1, /device:TPU:0, one launch (start us, length us, event | category | flops | bytes accessed | tf_op | source)
XLA Modules:
  0.0 952.9 jit_solution(11844844994991610371)
XLA Ops:
  25.6 36.1 %all_gather.22 = bf16[3,768,192]{2,0,1:T(4,128)(2,1)S(1)} all-gather(bf16[3,96,192]{2,0,1:T(4,128)(2,1)S(1)} %copy.66), channel_id=1, replica_groups=mesh['dp'=8,'tensor'=4] {'dp'}, dimensions={1}, use_global_device_ids=true | all-gather | bytes 995328 | tf_op jit(solution)/shard_map/all_gather | solution.py:129
  75.6 94.9 %while.27 = (s32[]{:T(128)}, bf16[4,512,3,64]{1,3,2,0:T(8,128)(2,1)}, f32[4,3,512]{2,1,0:T(4,128)}, s32[4,512]{1,0:T(4,128)S(1)}, s32[2048]{0:T(1024)S(1)}, /*in...) while((s32[]{:T(128)}, ...), condition=%wide.region_8.9_spmd, body=%wide.region_5.8_spmd.sunk | while | flops 834763264 | bytes 43974772 | solution.py:170
  76.5 7.6 select_reduce_fusion.3
  84.1 7.8 fusion.142
  91.9 7.0 fusion.143
  100.2 7.6 select_reduce_fusion.3
  107.8 7.8 fusion.142
  115.5 7.0 fusion.143
  123.8 7.6 select_reduce_fusion.3
  131.4 7.8 fusion.142
  139.2 7.0 fusion.143
  147.5 7.6 select_reduce_fusion.3
  155.1 7.8 fusion.142
  162.8 7.0 fusion.143
  184.5 29.4 %reduce-scatter.13.cloned.1.call-done = bf16[512,768]{1,0:T(8,128)(2,1)} async-done(((bf16[2048,768]{1,0:T(8,128)(2,1)}), bf16[512,768]{1,0:T(8,128)(2,1)}) %reduce-scatter.13.cloned.1.call-update) | async-done | bytes 786448 | tf_op jit(solution)/shard_map/reduce_scatter | solution.py:172
  222.0 27.2 %all-gather.9.cloned.1.call-done = bf16[2048,768]{1,0:T(8,128)(2,1)} async-done(((bf16[512,768]{1,0:T(8,128)(2,1)}), bf16[2048,768]{1,0:T(8,128)(2,1)}) %all-gather.9.cloned.1.call-update) | async-done | bytes 3145744 | tf_op jit(solution)/shard_map/all_gather | solution.py:182
  249.2 7.5 fusion.90
  256.7 36.0 %all-gather.13.cloned.1.call-done = bf16[768,768]{0,1:T(8,128)(2,1)} async-done(((bf16[768,96]{0,1:T(8,128)(2,1)}), bf16[768,768]{0,1:T(8,128)(2,1)}) %all-gather.13.cloned.1.call-update) | async-done | bytes 1179664 | tf_op jit(solution)/shard_map/all_gather | solution.py:132
  292.7 28.9 %all-gather.15.cloned.1.call-done = bf16[2048,768]{1,0:T(8,128)(2,1)} async-done(((bf16[512,768]{1,0:T(8,128)(2,1)}), bf16[2048,768]{1,0:T(8,128)(2,1)}) %all-gather.15.cloned.1.call-update) | async-done | bytes 3145744 | tf_op jit(solution)/shard_map/all_gather | solution.py:196
  321.7 10.8 %convert_reduce_fusion = (f32[768]{0:T(1024)}, bf16[2048,768]{1,0:T(8,128)(2,1)S(1)}, bf16[2048,768]{1,0:T(8,128)(2,1)}) fusion(f32[2048,768]{1,0:T(8,128)} %fusion.90, f32[768]{0:T(1024)S(1)} %dynamic_slice.28, bf16[2048,768]{1,0:T(8,128)(2,1)} %all-gather.15.cloned.1.call-done, bf16[768,768]{0,1:T(8,128)(2,1)} %all-gather.13.cloned.1.call-done), kind=kOutput, calls=%fused_computation.57 | convolution fusion | flops 2455239936 | bytes 16914432 | tf_op jit(solution)/shard_map/dot_general | solution.py:200
  339.4 6.2 convolution_convert_fusion.1
  345.8 30.4 %reduce-scatter.17.cloned.1.call-done = bf16[512,768]{1,0:T(8,128)(2,1)} async-done(((bf16[2048,768]{1,0:T(8,128)(2,1)}), bf16[512,768]{1,0:T(8,128)(2,1)}) %reduce-scatter.17.cloned.1.call-update) | async-done | bytes 786448 | tf_op jit(solution)/shard_map/reduce_scatter | solution.py:211
  380.2 36.4 %reduce-scatter.15.cloned.1.call-done = bf16[512,768]{1,0:T(8,128)(2,1)} async-done(((bf16[2048,768]{1,0:T(8,128)(2,1)}), bf16[512,768]{1,0:T(8,128)(2,1)}) %reduce-scatter.15.cloned.1.call-update) | async-done | bytes 786448 | tf_op jit(solution)/shard_map/reduce_scatter | solution.py:187
  423.8 28.4 %all-gather.17.cloned.1.call-done = bf16[2048,768]{1,0:T(8,128)(2,1)} async-done(((bf16[512,768]{1,0:T(8,128)(2,1)}), bf16[2048,768]{1,0:T(8,128)(2,1)}) %all-gather.17.cloned.1.call-update) | async-done | bytes 3145744 | tf_op jit(solution)/shard_map/all_gather | solution.py:230
  456.1 157.6 %while.28 = (s32[]{:T(128)}, f32[2048,3,64]{0,2,1:T(8,128)}, f32[2048,3,64]{0,2,1:T(8,128)}, f32[4,512,3,64]{1,0,3,2:T(4,128)}, bf16[4,512,3,64]{1,3,2,0:T(8,128...) while((s32[]{:T(128)}, f32[2048,3,64]{0,2,1:T(8,128)}, ...), condition=%wide.region_18.19_spmd.clone, body=%wide.region_16.18_spmd.clone.sunk | while | flops 2053634560 | bytes 151972176 | solution.py:264
  465.1 5.4 multiply_reduce_fusion.5
  470.5 5.9 multiply_convert_fusion.3
  485.5 8.6 dynamic_update_slice.24
  498.6 5.8 fusion.155
  504.3 5.4 multiply_reduce_fusion.5
  509.8 5.9 multiply_convert_fusion.3
  525.3 8.6 dynamic_update_slice.24
  538.4 5.8 fusion.155
  544.1 5.4 multiply_reduce_fusion.5
  549.6 5.9 multiply_convert_fusion.3
  565.1 8.6 dynamic_update_slice.24
  578.2 5.8 fusion.155
  589.4 5.9 multiply_convert_fusion.3
  604.9 8.6 dynamic_update_slice.24
  638.6 5.7 bitcast_convert_fusion
  646.2 6.0 fusion.91
  652.6 6.9 fusion.92
  666.6 19.2 %reduce-scatter.27.cloned.1.call-done = f32[96,192]{1,0:T(8,128)} async-done(((f32[768,192]{1,0:T(8,128)}), f32[96,192]{1,0:T(8,128)}) %reduce-scatter.27.cloned.1.call-update) | async-done | bytes 73744
  687.4 68.7 %reduce-scatter.25.cloned.1.call-done = f32[96,576]{1,0:T(8,128)} async-done(((f32[768,576]{1,0:T(8,128)}), f32[96,576]{1,0:T(8,128)}) %reduce-scatter.25.cloned.1.call-update) | async-done | bytes 221200
  758.0 37.5 %reduce-scatter.19.cloned.1.call-done = bf16[512,768]{1,0:T(8,128)(2,1)} async-done(((bf16[2048,768]{1,0:T(8,128)(2,1)}), bf16[512,768]{1,0:T(8,128)(2,1)}) %reduce-scatter.19.cloned.1.call-update) | async-done | bytes 786448 | tf_op jit(solution)/shard_map/reduce_scatter | solution.py:278
  798.0 41.6 %all-reduce = (f32[768]{0:T(1024)}, f32[768]{0:T(1024)}, f32[768]{0:T(1024)}, f32[3072]{0:T(1024)}, f32[768]{0:T(1024)}, /*index=5*/f32[2304]{0:T(1024)}) all-reduce(f32[768]{0:T(1024)S(1)} %get-tuple-element.311, f32[768]{0:T(1024)S(1)} %get-tuple-element.314, ...), channel_id=1, replica_groups=mesh['dp'=8,'tensor'=4] {'dp','tensor'}, use_global_device_ids=true, to_apply=%region_23.24 | all-reduce | flops 8448 | bytes 67584 | tf_op jit(solution)/shard_map/psum | solution.py:295
  842.9 27.2 %reduce-scatter.21.cloned.1.call-done = f32[96,768]{1,0:T(8,128)} async-done(((f32[768,768]{1,0:T(8,128)}), f32[96,768]{1,0:T(8,128)}) %reduce-scatter.21.cloned.1.call-update) | async-done | bytes 294928 | tf_op jit(solution)/shard_map/reduce_scatter | solution.py:292
  870.1 72.9 %reduce-scatter.23.cloned.1.call-done = f32[768,96]{0,1:T(8,128)} async-done(((f32[768,768]{0,1:T(8,128)}), f32[768,96]{0,1:T(8,128)}) %reduce-scatter.23.cloned.1.call-update) | async-done | bytes 294928 | tf_op jit(solution)/shard_map/reduce_scatter | solution.py:293
  (338 shorter events, 191.3 us)
Async XLA Ops:
  8.0 171.3 %copy-start = (f32[128,2304]{1,0:T(8,128)S(1)}, f32[128,2304]{1,0:T(8,128)}, u32[]{:S(2)}) copy-start(f32[128,2304]{1,0:T(8,128)} %param.32) | copy-start | bytes 3538948
  8.1 57.2 %all-gather.7.cloned.1.call-start = ((), (), s32[]{:S(2)}) async-start(), calls=%async_computation.8 | async-start | bytes 3932160 | tf_op jit(solution)/shard_map/all_gather | solution.py:138
  10.3 5.1 copy-start.60
  12.3 9.3 copy-start.37
  12.3 201.5 %reduce-scatter.13.cloned.1.call-start = ((), (), s32[]{:S(2)}) async-start(), calls=%async_computation.9 | async-start | bytes 3932160 | tf_op jit(solution)/shard_map/reduce_scatter | solution.py:172
  12.4 5.1 collective-permute-start
  17.6 4.8 collective-permute-start.1
  22.5 41.3 %collective-permute-start.2 = (bf16[4,192,96]{2,1,0:T(8,128)(2,1)S(1)}, bf16[4,192,96]{2,1,0:T(8,128)(2,1)S(1)}, u32[]{:S(2)}, u32[]{:S(2)}) collective-permute-start(bf16[4,192,96]{2,1,0:T(8,128)(2,1)S(1)} %bitcast.188), channel_id=1, source_target_pairs={{0,16},{4,20},{8,24},{12,28},{16,0},{20,4},{24,8},{28,12},{1,17},{... | collective-permute-start | bytes 442376 | tf_op jit(solution)/shard_map/ppermute | solution.py:23
  170.5 5.8 copy-start.11
  176.4 45.7 %all-gather.11.cloned.1.call-start = ((), (), s32[]{:S(2)}) async-start(), calls=%async_computation.11 | async-start | bytes 1327104 | tf_op jit(solution)/shard_map/all_gather | solution.py:131
  178.0 71.3 %all-gather.9.cloned.1.call-start = ((), (), s32[]{:S(2)}) async-start(), calls=%async_computation.10 | async-start | bytes 3932160 | tf_op jit(solution)/shard_map/all_gather | solution.py:182
  180.0 33.8 %copy-start.8 = (f32[512,768]{1,0:T(8,128)S(1)}, f32[512,768]{1,0:T(8,128)}, u32[]{:S(2)}) copy-start(f32[512,768]{1,0:T(8,128)} %param.19) | copy-start | bytes 4718596
  180.0 33.8 %copy-start.58 = (f32[768]{0:T(1024)S(1)}, f32[768]{0:T(1024)}, u32[]{:S(2)}) copy-start(f32[768]{0:T(1024)} %param.27) | copy-start | bytes 9220
  219.7 73.1 %all-gather.13.cloned.1.call-start = ((), (), s32[]{:S(2)}) async-start(), calls=%async_computation.12 | async-start | bytes 1327104 | tf_op jit(solution)/shard_map/all_gather | solution.py:132
  220.4 101.2 %all-gather.15.cloned.1.call-start = ((), (), s32[]{:S(2)}) async-start(), calls=%async_computation.14 | async-start | bytes 3932160 | tf_op jit(solution)/shard_map/all_gather | solution.py:196
  221.2 155.0 %reduce-scatter.17.cloned.1.call-start = ((), (), s32[]{:S(2)}) async-start(), calls=%async_computation.15 | async-start | bytes 3932160 | tf_op jit(solution)/shard_map/reduce_scatter | solution.py:211
  256.7 77.4 %copy-start.63 = (bf16[768,768]{1,0:T(8,128)(2,1)S(1)}, bf16[768,768]{1,0:T(8,128)(2,1)}, u32[]{:S(2)}) copy-start(bf16[768,768]{1,0:T(8,128)(2,1)} %all-gather.11.cloned.1.call-done) | copy-start | bytes 3538948
  338.2 78.3 %reduce-scatter.15.cloned.1.call-start = ((), (), s32[]{:S(2)}) async-start(), calls=%async_computation.13 | async-start | bytes 3932160 | tf_op jit(solution)/shard_map/reduce_scatter | solution.py:187
  345.7 30.5 %copy-start.13 = (f32[512,768]{1,0:T(8,128)S(1)}, f32[512,768]{1,0:T(8,128)}, u32[]{:S(2)}) copy-start(f32[512,768]{1,0:T(8,128)} %copy-done.12) | copy-start | bytes 4718596
  345.7 70.8 %copy-start.59 = (f32[768]{0:T(1024)S(1)}, f32[768]{0:T(1024)}, u32[]{:S(2)}) copy-start(f32[768]{0:T(1024)} %param.31) | copy-start | bytes 9220
  345.7 106.5 %all-gather.17.cloned.1.call-start = ((), (), s32[]{:S(2)}) async-start(), calls=%async_computation.16 | async-start | bytes 3932160 | tf_op jit(solution)/shard_map/all_gather | solution.py:230
  376.2 40.3 %copy-start.17 = (bf16[512,768]{1,0:T(8,128)(2,1)S(1)}, bf16[512,768]{1,0:T(8,128)(2,1)}, u32[]{:S(2)}) copy-start(bf16[512,768]{1,0:T(8,128)(2,1)} %reduce-scatter.17.cloned.1.call-done) | copy-start | bytes 2359300
  421.6 30.6 %copy-start.28 = (bf16[192,768]{1,0:T(8,128)(2,1)S(1)}, bf16[192,768]{1,0:T(8,128)(2,1)}, u32[]{:S(2)}) copy-start(bf16[192,768]{1,0:T(8,128)(2,1)} %reshape.322) | copy-start | bytes 884740
  423.8 262.0 %reduce-scatter.27.cloned.1.call-start = ((), (), s32[]{:S(2)}) async-start(), calls=%async_computation.22 | async-start | bytes 884736
  476.4 5.1 copy-start.2
  481.5 12.6 %copy-start.5 = (bf16[2048,3,64]{0,2,1:T(8,128)(2,1)S(1)}, bf16[2048,3,64]{0,2,1:T(8,128)(2,1)}, u32[]{:S(2)}) copy-start(bf16[2048,3,64]{0,2,1:T(8,128)(2,1)} %copy-done.4) | copy-start | bytes 2359300 | tf_op jit(solution)/shard_map/while
  481.5 12.6 %copy-start.16 = (bf16[4,512,3,64]{1,3,2,0:T(8,128)(2,1)S(1)}, bf16[4,512,3,64]{1,3,2,0:T(8,128)(2,1)}, u32[]{:S(2)}) copy-start(bf16[4,512,3,64]{1,3,2,0:T(8,128)(2,1)} %copy-done.15) | copy-start | bytes 2359300 | tf_op jit(solution)/shard_map/while
  515.6 5.1 copy-start.2
  520.8 13.1 %copy-start.5 = (bf16[2048,3,64]{0,2,1:T(8,128)(2,1)S(1)}, bf16[2048,3,64]{0,2,1:T(8,128)(2,1)}, u32[]{:S(2)}) copy-start(bf16[2048,3,64]{0,2,1:T(8,128)(2,1)} %copy-done.4) | copy-start | bytes 2359300 | tf_op jit(solution)/shard_map/while
  520.8 13.1 %copy-start.16 = (bf16[4,512,3,64]{1,3,2,0:T(8,128)(2,1)S(1)}, bf16[4,512,3,64]{1,3,2,0:T(8,128)(2,1)}, u32[]{:S(2)}) copy-start(bf16[4,512,3,64]{1,3,2,0:T(8,128)(2,1)} %copy-done.15) | copy-start | bytes 2359300 | tf_op jit(solution)/shard_map/while
  560.6 13.1 %copy-start.5 = (bf16[2048,3,64]{0,2,1:T(8,128)(2,1)S(1)}, bf16[2048,3,64]{0,2,1:T(8,128)(2,1)}, u32[]{:S(2)}) copy-start(bf16[2048,3,64]{0,2,1:T(8,128)(2,1)} %copy-done.4) | copy-start | bytes 2359300 | tf_op jit(solution)/shard_map/while
  560.6 13.1 %copy-start.16 = (bf16[4,512,3,64]{1,3,2,0:T(8,128)(2,1)S(1)}, bf16[4,512,3,64]{1,3,2,0:T(8,128)(2,1)}, u32[]{:S(2)}) copy-start(bf16[4,512,3,64]{1,3,2,0:T(8,128)(2,1)} %copy-done.15) | copy-start | bytes 2359300 | tf_op jit(solution)/shard_map/while
  595.3 5.1 copy-start.2
  600.4 13.1 %copy-start.5 = (bf16[2048,3,64]{0,2,1:T(8,128)(2,1)S(1)}, bf16[2048,3,64]{0,2,1:T(8,128)(2,1)}, u32[]{:S(2)}) copy-start(bf16[2048,3,64]{0,2,1:T(8,128)(2,1)} %copy-done.4) | copy-start | bytes 2359300 | tf_op jit(solution)/shard_map/while
  600.4 13.1 %copy-start.16 = (bf16[4,512,3,64]{1,3,2,0:T(8,128)(2,1)S(1)}, bf16[4,512,3,64]{1,3,2,0:T(8,128)(2,1)}, u32[]{:S(2)}) copy-start(bf16[4,512,3,64]{1,3,2,0:T(8,128)(2,1)} %copy-done.15) | copy-start | bytes 2359300 | tf_op jit(solution)/shard_map/while
  622.1 134.0 %reduce-scatter.25.cloned.1.call-start = ((), (), s32[]{:S(2)}) async-start(), calls=%async_computation.21 | async-start | bytes 2211840
  637.3 158.2 %reduce-scatter.19.cloned.1.call-start = ((), (), s32[]{:S(2)}) async-start(), calls=%async_computation.17 | async-start | bytes 3932160 | tf_op jit(solution)/shard_map/reduce_scatter | solution.py:278
  644.4 225.7 %reduce-scatter.21.cloned.1.call-start = ((), (), s32[]{:S(2)}) async-start(), calls=%async_computation.18 | async-start | bytes 2654208 | tf_op jit(solution)/shard_map/reduce_scatter | solution.py:292
  652.3 290.7 %reduce-scatter.23.cloned.1.call-start = ((), (), s32[]{:S(2)}) async-start(), calls=%async_computation.19 | async-start | bytes 2654208 | tf_op jit(solution)/shard_map/reduce_scatter | solution.py:293
  659.5 283.4 %all-reduce.3.cloned.1.call-start = ((), (), s32[]{:S(2)}) async-start(), calls=%async_computation.20 | async-start | bytes 2359296 | tf_op jit(solution)/shard_map/psum | solution.py:295
  664.3 131.1 %copy-start.9 = (f32[512,768]{1,0:T(8,128)S(1)}, f32[512,768]{1,0:T(8,128)}, u32[]{:S(2)}) copy-start(f32[512,768]{1,0:T(8,128)} %param.19) | copy-start | bytes 4718596
  664.4 131.1 %copy-start.46 = (f32[512]{0:T(512)S(1)}, f32[512]{0:T(512)}, u32[]{:S(2)}) copy-start(f32[512]{0:T(512)} %copy-done.45) | copy-start | bytes 6148
  664.4 131.1 %copy-start.48 = (f32[768]{0:T(1024)S(1)}, f32[768]{0:T(1024)}, u32[]{:S(2)}) copy-start(f32[768]{0:T(1024)} %param.23) | copy-start | bytes 9220
  664.4 131.1 %copy-start.50 = (f32[512]{0:T(512)S(1)}, f32[512]{0:T(512)}, u32[]{:S(2)}) copy-start(f32[512]{0:T(512)} %copy-done.49) | copy-start | bytes 6148
  687.4 110.6 %copy-start.51 = (f32[768]{0:T(1024)S(1)}, f32[768]{0:T(1024)}, u32[]{:S(2)}) copy-start(f32[768]{0:T(1024)} %get-tuple-element.310) | copy-start | bytes 9220
  687.4 110.6 %copy-start.52 = (f32[768]{0:T(1024)S(1)}, f32[768]{0:T(1024)}, u32[]{:S(2)}) copy-start(f32[768]{0:T(1024)} %get-tuple-element.363) | copy-start | bytes 9220
  795.5 44.2 %copy-start.21 = (bf16[512,768]{1,0:T(8,128)(2,1)S(1)}, bf16[512,768]{1,0:T(8,128)(2,1)}, u32[]{:S(2)}) copy-start(bf16[512,768]{1,0:T(8,128)(2,1)} %reduce-scatter.19.cloned.1.call-done) | copy-start | bytes 2359300
  839.7 105.7 %copy-start.1 = (f32[128,2304]{1,0:T(8,128)S(1)}, f32[128,2304]{1,0:T(8,128)}, u32[]{:S(2)}) copy-start(f32[128,2304]{1,0:T(8,128)} %param.32) | copy-start | bytes 3538948
  (55 other events, 134.9 us)
Sparse Core Ops, SparseCore 0:
  12.5 31.2 all-gather.6
  176.5 37.3 reduce-scatter.12
  338.3 37.8 reduce-scatter.16
  378.6 37.8 reduce-scatter.14
  666.7 151.9 all-reduce.2
Sparse Core Ops, SparseCore 1:
  179.6 40.8 all-gather.10
  222.5 26.7 all-gather.8
  251.3 41.4 all-gather.12
  294.9 26.7 all-gather.14
  423.8 28.4 all-gather.16
  622.2 63.6 reduce-scatter.26
  689.1 66.9 reduce-scatter.24
  758.5 36.9 reduce-scatter.18
  799.4 70.6 reduce-scatter.20
  874.2 68.7 reduce-scatter.22
